TPU v7x, 32 devices: a whole 2x2x4 slice. The times are simulated.
32 devices in a mesh: tm: 16 (over z, y, x), space: 2 (over core).
Axes of the slice: x: 2, y: 2, z: 4, core: 2. Of those that a mesh axis runs over, the one named last changes fastest.
Arguments:
- initial: float32 [16, 32, 64, 128], P('tm', 'space'), may hold values from -6 to 6
- source: float32 [16, 32, 64, 128], P('tm', 'space'), may hold values from -6 to 6
- diffusion: float32 [32, 64, 128], P('space'), may hold values from 0.1 to 1
- advection: float32 [3, 32, 64, 128], P(None, 'space'), may hold values from 0.05 to 0.5
Outputs:
- smoothed: float32 [16, 32, 64, 128], P('tm', 'space')
- residual: float32 [16, 32, 64, 128], P('tm', 'space')
All inputs are finite; a program needn't handle non-finite values.
Results may differ from a plain program's by a relative error of at most 0.00002.
Values sent between devices are 32-bit elements; how exact they have to be, the bound alone decides.
A program may use at most 64 MiB of HBM per device.

v0:
```python
import functools

import jax
import jax.numpy as jnp
from jax import lax
from jax.experimental import pallas as pl
from jax.experimental.pallas import tpu as pltpu
from jax.sharding import PartitionSpec as P

SWEEPS = 2
ITERS = 4
HALO = ITERS
VMEM_BYTES = 67043328
MESH = pl.DeviceIdType.MESH


def cuts(edges):
    return list(zip(edges[:-1], edges[1:]))


def plan(planes, step):
    arrive = list(range(0, planes, step)) + [planes]
    ready = lambda edges: [e if e == planes else max(e - (ITERS - 1), 0) for e in edges]
    split = lambda edges, most: sorted({c for a, b in cuts(edges) for c in list(range(a, b, most)) + [b]})
    first = cuts(arrive)
    second = cuts(split(sorted(set(ready(arrive))), step))
    edges = [0] + [b for _, b in second]
    third = cuts(split(sorted(set(ready(edges))), 2))
    return first, second, third


def kernel(planes, steps, sends, initial, source, diffusion, advection, s2, left, p3,
           v0, v1, v2, v3, s1, src, p1, p2, spread, upwind,
           low_z, high_z, low_x, high_x, low_y, high_y, inverse, diagonal, forced,
           load_sem, send1, recv1, send2, recv2, send3, recv3, hsend, hrecv):
    first, second, third = sends
    time, side = lax.axis_index("tm"), lax.axis_index("space")
    after, before = lax.rem(time + 1, steps), lax.rem(time + steps - 1, steps)
    other = 1 - side
    rows, lanes = v0.shape[1], v0.shape[2]

    def begin(lo, hi, who=side):
        return who * (HALO + lo) + (1 - who) * (HALO + planes - hi)

    def span(lo, hi, who=side):
        return pl.ds(begin(lo, hi, who), hi - lo)

    def grid_span(lo, hi):
        return pl.ds(begin(lo, hi) - HALO, hi - lo)

    barrier = pltpu.get_barrier_semaphore()
    for peer in ((before, side), (time, other)):
        pl.semaphore_signal(barrier, inc=1, device_id=peer, device_id_type=MESH)

    inner = pl.ds(HALO, planes)
    loads = [
        pltpu.make_async_copy(diffusion, spread.at[inner], load_sem.at[0]),
        pltpu.make_async_copy(advection, upwind.at[:, inner], load_sem.at[1]),
        pltpu.make_async_copy(source.at[0], src.at[inner], load_sem.at[2]),
        pltpu.make_async_copy(initial.at[0], v0.at[inner], load_sem.at[3]),
    ]
    for load in loads:
        load.start()

    edge = begin(planes, planes + 1)
    for field in (v0, v1, v2, v3, s1, s2):
        field[edge] = jnp.zeros((rows, lanes), jnp.float32)

    def forward(source_ref, target_ref, send, recv):
        return pltpu.make_async_remote_copy(
            src_ref=source_ref, dst_ref=target_ref, send_sem=send, recv_sem=recv,
            device_id=(after, side), device_id_type=MESH)

    def across(source_ref, target_ref, n):
        return pltpu.make_async_remote_copy(
            src_ref=source_ref, dst_ref=target_ref, send_sem=hsend.at[n], recv_sem=hrecv.at[n],
            device_id=(time, other), device_id_type=MESH)

    def rim(field, width, n):
        return across(field.at[span(0, width)], field.at[span(-width, 0, other)], n)

    near = HALO - 1
    sent1 = [
        forward(initial.at[0, grid_span(lo, hi)], p1.at[span(lo, hi)], send1.at[k], recv1.at[k])
        for k, (lo, hi) in enumerate(first)
    ]
    sent2 = [
        forward(s1.at[span(lo, hi)], p2.at[span(lo, hi)], send2.at[k], recv2.at[k])
        for k, (lo, hi) in enumerate(second)
    ]
    sent3 = [
        forward(s2.at[span(lo, hi)], p3.at[span(lo, hi)], send3.at[k], recv3.at[k])
        for k, (lo, hi) in enumerate(third)
    ]
    rims = [
        across(diffusion.at[grid_span(0, near)], spread.at[span(-near, 0, other)], 0),
        across(advection.at[:, grid_span(0, near)], upwind.at[:, span(-near, 0, other)], 1),
        across(source.at[0, grid_span(0, near)], src.at[span(-near, 0, other)], 2),
        across(initial.at[0, grid_span(0, HALO)], v0.at[span(-HALO, 0, other)], 3),
    ]
    rim_p1, rim_s1, rim_p2, rim_s2 = rim(p1, near, 4), rim(s1, HALO, 5), rim(p2, near, 6), rim(s2, 1, 7)

    pl.semaphore_wait(barrier, 2)
    sent1[0].start()
    for copy in rims:
        copy.start()
    for copy in sent1[1:]:
        copy.start()

    def each(lo, hi, body):
        if hi > lo:
            start = begin(lo, hi)

            def one(k, carry):
                body(start + k)
                return carry

            lax.fori_loop(0, hi - lo, one, 0)

    def coefficients(i):
        d = spread[i]
        ax, ay, az = upwind[0, i], upwind[1, i], upwind[2, i]
        main = 1.0 + 6.0 * d + (ax + ay + az)
        inv = 1.0 / main
        row = lax.broadcasted_iota(jnp.int32, (rows, lanes), 0)
        lane = lax.broadcasted_iota(jnp.int32, (rows, lanes), 1)
        even = d * inv
        high_z[i] = even
        low_z[i] = (d + az) * inv
        high_x[i] = jnp.where(row == rows - 1, 0.0, even)
        low_x[i] = jnp.where(row == 0, 0.0, (d + ax) * inv)
        high_y[i] = jnp.where(lane == lanes - 1, 0.0, even)
        low_y[i] = jnp.where(lane == 0, 0.0, (d + ay) * inv)
        inverse[i] = inv
        diagonal[i] = main

    def neighbours(v, i):
        here = v[i]
        total = low_z[i] * v[i - 1] + high_z[i] * v[i + 1]
        total += low_x[i] * pltpu.roll(here, 1, 0) + high_x[i] * pltpu.roll(here, rows - 1, 0)
        return total + (low_y[i] * pltpu.roll(here, 1, 1) + high_y[i] * pltpu.roll(here, lanes - 1, 1))

    def sweep(start, target, prior, arrivals, ranges, rim_prior, on_ready):
        levels = [start, v1, v2, v3, target]
        reached = [-near] + [-(ITERS - n) for n in range(1, ITERS + 1)]
        rimmed = False
        for k, (lo, hi) in enumerate(ranges):
            arrivals[k].wait_recv()
            if hi < near:
                continue
            if not rimmed:
                rim_prior.start()
                rim_prior.wait_recv()
                rimmed = True
            goal = hi

            def force(i):
                forced[i] = (prior[i] + src[i]) * inverse[i]

            each(reached[0], goal, force)
            reached[0] = goal
            for n in range(1, ITERS + 1):
                goal = hi if hi == planes else hi - (n - 1)

                def iterate(i, n=n):
                    levels[n][i] = forced[i] + neighbours(levels[n - 1], i)

                each(reached[n], goal, iterate)
                reached[n] = max(reached[n], goal)
            on_ready(reached[ITERS])

    for n in (0, 1):
        loads[n].wait()
        rims[n].wait_recv()
    each(-near, planes, coefficients)
    for n in (2, 3):
        loads[n].wait()
        rims[n].wait_recv()

    issued = {"s1": 0, "s2": 0, "rim": set()}

    def issue(name, copies, ranges, ready):
        while issued[name] < len(ranges) and ranges[issued[name]][1] <= ready:
            copies[issued[name]].start()
            issued[name] += 1

    def first_ready(ready):
        if ready >= HALO and "s1" not in issued["rim"]:
            issued["rim"].add("s1")
            rim_s1.start()
        issue("s1", sent2, second, ready)

    def second_ready(ready):
        if ready >= 1 and "s2" not in issued["rim"]:
            issued["rim"].add("s2")
            rim_s2.start()
        issue("s2", sent3, third, ready)

    sweep(v0, s1, p1, sent1, first, rim_p1, first_ready)
    rim_s1.wait_recv()
    sweep(s1, s2, p2, sent2, second, rim_p2, second_ready)
    rim_s2.wait_recv()

    def partial(i):
        left[i] = src[i] - diagonal[i] * (s2[i] - neighbours(s2, i))

    each(0, planes, partial)

    for copy in sent3:
        copy.wait_recv()
    for copy in rims + [rim_p1, rim_s1, rim_p2, rim_s2] + sent1 + sent2 + sent3:
        copy.wait_send()


def finish(planes, step, s2, left, p3, smoothed, residual, total, sem):
    out = pltpu.make_async_copy(s2.at[pl.ds(HALO, planes)], smoothed.at[0], sem.at[0])
    out.start()
    copies = [out]
    for k, lo in enumerate(range(0, planes, step)):
        size = min(step, planes - lo)
        part, wide = pl.ds(lo, size), pl.ds(HALO + lo, size)
        total[part] = left[wide] + p3[wide]
        copies.append(pltpu.make_async_copy(total.at[part], residual.at[0, part], sem.at[1 + k]))
        copies[-1].start()
    for copy in copies:
        copy.wait()


def body(steps, sides, initial, source, diffusion, advection):
    assert sides == 2
    _, planes, rows, lanes = initial.shape
    sends = plan(planes, 4)
    shape = (planes + 2 * HALO, rows, lanes)
    wide = pltpu.VMEM(shape, jnp.float32)
    triple = pltpu.VMEM((3,) + shape, jnp.float32)
    dma = pltpu.SemaphoreType.DMA
    pairs = [dma((len(s),)) for s in sends for _ in range(2)]
    result = jax.ShapeDtypeStruct(initial.shape, jnp.float32)
    vmem = pl.BlockSpec(memory_space=pltpu.VMEM)
    hbm = pl.BlockSpec(memory_space=pltpu.HBM)
    grant = VMEM_BYTES - (3 * shape[0] + 4) * rows * lanes * 4
    held = pl.pallas_call(
        functools.partial(kernel, planes, steps, sends),
        out_shape=(wide,) * 3,
        in_specs=[hbm] * 4,
        out_specs=(vmem,) * 3,
        scratch_shapes=[wide] * 9 + [triple] + [wide] * 9
        + [dma((4,))] + pairs + [dma((8,)), dma((8,))],
        compiler_params=pltpu.CompilerParams(collective_id=0, has_side_effects=True, vmem_limit_bytes=grant),
        name="smooth",
    )(initial, source, diffusion, advection)
    step = 4
    return pl.pallas_call(
        functools.partial(finish, planes, step),
        out_shape=(result, result),
        in_specs=[vmem] * 3,
        out_specs=(hbm,) * 2,
        scratch_shapes=[pltpu.VMEM((planes, rows, lanes), jnp.float32), dma((1 + -(-planes // step),))],
        compiler_params=pltpu.CompilerParams(vmem_limit_bytes=8 << 20),
        name="finish",
    )(*held)


def solution(mesh):
    in_specs = (
        P("tm", "space", None, None),
        P("tm", "space", None, None),
        P("space", None, None),
        P(None, "space", None, None),
    )
    out_specs = (P("tm", "space", None, None), P("tm", "space", None, None))
    run = functools.partial(body, mesh.shape["tm"], mesh.shape["space"])
    return jax.shard_map(run, mesh=mesh, in_specs=in_specs, out_specs=out_specs, check_vma=False)
```

profile of v0, /device:TPU:0, one launch (start us, length us, event | category | flops | bytes accessed | tf_op | source)
XLA Modules:
  0.0 44.4 jit_solution(1171554435407945485)
XLA Ops:
  0.6 42.8 %smooth.1 = (f32[24,64,128]{2,1,0:T(8,128)S(1)}, f32[24,64,128]{2,1,0:T(8,128)S(1)}, f32[24,64,128]{2,1,0:T(8,128)S(1)}) custom-call(f32[1,16,64,128]{3,2,1,0:T(8,128)} %initial.1, f32[1,16,64,128]{3,2,1,0:T(8,128)} %source.1, f32[16,64,128]{2,1,0:T(8,128)} %diffusion.1, f32[3,16,64,128]{3,2,1,0:T(8,128)} %advection.1), custom_call_target="tpu_custom_call" | custom-call | tf_op jit(solution)/shard_map/smooth/pallas_call | solution.py:242
  43.4 1.0 %finish.1 = (f32[1,16,64,128]{3,2,1,0:T(8,128)}, f32[1,16,64,128]{3,2,1,0:T(8,128)}) custom-call(f32[24,64,128]{2,1,0:T(8,128)S(1)} %get-tuple-element.5.s2, f32[24,64,128]{2,1,0:T(8,128)S(1)} %get-tuple-element.6.left, f32[24,64,128]{2,1,0:T(8,128)S(1)} %get-tuple-element.7.p3), custom_call_target="tpu_custom_call" | custom-call | tf_op jit(solution)/shard_map/finish/pallas_call | solution.py:253
where the time goes:
time: 44.6 us; the launch traced here: 44.4 us
  Pallas kernels  43.8 us (98%)
  between operations  0.64 us (1%)
    pallas_call x1, Pallas kernels, body(): pl.pallas_call(functools.partial(kernel, planes, steps, sends), out_shape...  42.8 us
    pallas_call x1, Pallas kernels, body(): pl.pallas_call(functools.partial(finish, planes, step), out_shape=(result...  1 us

commit v1 on v0

v1 whole, which is shorter than its diff:
```python
import functools

import jax
import jax.numpy as jnp
from jax import lax
from jax.experimental import pallas as pl
from jax.experimental.pallas import tpu as pltpu
from jax.sharding import PartitionSpec as P

ITERS = 4
HALO = ITERS
STEP = 2
LAG = 3
VMEM_BYTES = 67043328
MESH = pl.DeviceIdType.MESH


def kernel(planes, steps, relayed, initial, source, diffusion, advection, s2, res,
           u, src, spread, upwind, low_z, high_z, low_x, high_x, low_y, high_y, inverse, diagonal,
           base, forced, y0, y1, y2, y3, v1, v2, v3, g, e, z, e_in, z_in, r, p3,
           load_sem, send_e, recv_e, send_z, recv_z, send_s, recv_s, send_f, hsend, hrecv):
    count = planes // STEP
    half = planes // 2
    time, side = lax.axis_index("tm"), lax.axis_index("space")
    odd = lax.rem(time, 2)
    partner = time + 1 - 2 * odd
    after, before = lax.rem(time + 1, steps), lax.rem(time + steps - 1, steps)
    beyond, behind = lax.rem(time + 2, steps), lax.rem(time + steps - 2, steps)
    other = 1 - side
    rows, lanes = u.shape[1], u.shape[2]

    def begin(lo, hi, who=side):
        return (1 - who) * (HALO + lo) + who * (HALO + planes - hi)

    def span(lo, hi, who=side):
        return pl.ds(begin(lo, hi, who), hi - lo if isinstance(lo, int) else STEP)

    def grid_span(lo, hi):
        return pl.ds(begin(lo, hi) - HALO, hi - lo)

    def part(k):
        return pl.ds(begin(STEP * k, STEP * k + STEP), STEP)

    barrier = pltpu.get_barrier_semaphore()
    for peer in ((partner, side), (behind, side), (before, side), (time, other)):
        pl.semaphore_signal(barrier, inc=1, device_id=peer, device_id_type=MESH)

    loads = []
    for n, (lo, hi) in enumerate(((0, half), (half, planes))):
        here, there = span(lo, hi), grid_span(lo, hi)
        loads.append([
            pltpu.make_async_copy(diffusion.at[there], spread.at[here], load_sem.at[n, 0]),
            pltpu.make_async_copy(advection.at[:, there], upwind.at[:, here], load_sem.at[n, 1]),
            pltpu.make_async_copy(initial.at[0, there], u.at[here], load_sem.at[n, 2]),
            pltpu.make_async_copy(source.at[0, there], src.at[here], load_sem.at[n, 3]),
        ])
    for group in loads:
        for load in group:
            load.start()

    edge = begin(-1, 0)
    for field in (u, y0, y1, y2, y3, v1, v2, v3, g, s2):
        field[edge] = jnp.zeros((rows, lanes), jnp.float32)

    def across(source_ref, target_ref, n):
        return pltpu.make_async_remote_copy(
            src_ref=source_ref, dst_ref=target_ref, send_sem=hsend.at[n], recv_sem=hrecv.at[n],
            device_id=(time, other), device_id_type=MESH)

    def rim(field, width, n):
        return across(field.at[span(planes - width, planes)],
                      field.at[span(planes, planes + width, other)], n)

    mine, theirs = grid_span(planes - HALO, planes), span(planes, planes + HALO, other)
    rims = [
        across(diffusion.at[mine], spread.at[theirs], 0),
        across(advection.at[:, mine], upwind.at[:, theirs], 1),
        across(initial.at[0, mine], u.at[theirs], 2),
        across(source.at[0, mine], src.at[theirs], 3),
    ]
    rim_g, rim_r, rim_s = rim(g, HALO, 4), rim(r, HALO - 1, 5), rim(s2, 1, 6)

    def swap(k):
        return pltpu.make_async_remote_copy(
            src_ref=e.at[part(k)], dst_ref=e_in.at[part(k)], send_sem=send_e.at[k], recv_sem=recv_e.at[k],
            device_id=(partner, side), device_id_type=MESH)

    def hand(k):
        return pltpu.make_async_remote_copy(
            src_ref=z.at[part(k)], dst_ref=z_in.at[part(k)], send_sem=send_z.at[k], recv_sem=recv_z.at[k],
            device_id=(beyond, side), device_id_type=MESH)

    def pass_on(m):
        detour = odd * jnp.where(m < relayed, 1, 0)
        return pltpu.make_async_remote_copy(
            src_ref=s2.at[part(m)], dst_ref=p3.at[detour, part(m)], send_sem=send_s.at[m],
            recv_sem=recv_s.at[detour, m],
            device_id=(jnp.where(detour == 1, beyond, after), side), device_id_type=MESH)

    def forward(m):
        return pltpu.make_async_remote_copy(
            src_ref=p3.at[1, part(m)], dst_ref=p3.at[0, part(m)], send_sem=send_f.at[m],
            recv_sem=recv_s.at[0, m], device_id=(before, side), device_id_type=MESH)

    def detoured(m):
        return pltpu.make_async_remote_copy(
            src_ref=s2.at[part(m)], dst_ref=p3.at[1, part(m)], send_sem=send_s.at[m],
            recv_sem=recv_s.at[1, m], device_id=(beyond, side), device_id_type=MESH)

    def arrival(m):
        return pltpu.make_async_remote_copy(
            src_ref=s2.at[part(m)], dst_ref=p3.at[0, part(m)], send_sem=send_s.at[m],
            recv_sem=recv_s.at[0, m], device_id=(after, side), device_id_type=MESH)

    def each(lo, hi, body):
        start = begin(lo, hi)
        for k in range(hi - lo):
            body(start + k)

    def pair(lo, body):
        start = begin(lo, lo + STEP)
        for k in range(STEP):
            body(start + k)

    row = lax.broadcasted_iota(jnp.int32, (rows, lanes), 0)
    lane = lax.broadcasted_iota(jnp.int32, (rows, lanes), 1)

    def coefficients(i):
        d = spread[i]
        ax, ay, az = upwind[0, i], upwind[1, i], upwind[2, i]
        main = 1.0 + 6.0 * d + (ax + ay + az)
        inv = 1.0 / main
        even = d * inv
        high_z[i] = even
        low_z[i] = (d + az) * inv
        high_x[i] = jnp.where(row == rows - 1, 0.0, even)
        low_x[i] = jnp.where(row == 0, 0.0, (d + ax) * inv)
        high_y[i] = jnp.where(lane == lanes - 1, 0.0, even)
        low_y[i] = jnp.where(lane == 0, 0.0, (d + ay) * inv)
        inverse[i] = inv
        diagonal[i] = main
        y0[i] = u[i] * inv
        base[i] = src[i] * inv

    def neighbours(v, i):
        here = v[i]
        total = low_z[i] * v[i - 1] + high_z[i] * v[i + 1]
        total += low_x[i] * pltpu.roll(here, 1, 0) + high_x[i] * pltpu.roll(here, rows - 1, 0)
        return total + (low_y[i] * pltpu.roll(here, 1, 1) + high_y[i] * pltpu.roll(here, lanes - 1, 1))

    powers, bases = [y0, y1, y2, y3], [u, v1, v2, v3]

    def lift(n):
        def one(i):
            y = neighbours(powers[n - 1], i)
            b = base[i] + neighbours(bases[n - 1], i)
            if n < ITERS:
                powers[n][i] = y
                bases[n][i] = b
            else:
                g[i] = b
                e[i] = b + diagonal[i] * y
                z[i] = (y0[i] + y1[i]) + (y2[i] + y3[i])
        return one

    def emit(k):
        swap(k).start()

        @pl.when(odd == 1)
        def _():
            hand(k).start()

    for load in loads[0]:
        load.wait()
    each(0, STEP + ITERS, coefficients)
    for n in range(1, ITERS + 1):
        each(0, STEP + ITERS - n, lift(n))
    pl.semaphore_wait(barrier, 4)
    emit(0)
    for copy in rims:
        copy.start()

    def local(k, carry):
        lo = STEP * k

        @pl.when(lo + ITERS == half)
        def _():
            for load in loads[1]:
                load.wait()

        @pl.when(lo + ITERS == planes)
        def _():
            for copy in rims:
                copy.wait_recv()

        pair(lo + ITERS, coefficients)
        for n in range(1, ITERS + 1):
            pair(lo + ITERS - n, lift(n))
        emit(k)
        return carry

    lax.fori_loop(1, count, local, 0)
    rim_g.start()

    def combine(k):
        @pl.when(odd == 0)
        def _():
            swap(k).wait_recv()

            def one(i):
                z[i] = z[i] + e_in[i]

            pair(STEP * k, one)
            hand(k).start()

    levels = [g, v1, v2, v3, s2]

    def force(i):
        forced[i] = (src[i] + r[i]) * inverse[i]

    def iterate(n):
        def one(i):
            levels[n][i] = forced[i] + neighbours(levels[n - 1], i)
        return one

    def gather(k):
        hand(k).wait_recv()

        @pl.when(odd == 1)
        def _():
            swap(k).wait_recv()

            def one(i):
                r[i] = z_in[i] + e_in[i]

            pair(STEP * k, one)

        @pl.when(odd == 0)
        def _():
            def one(i):
                r[i] = z_in[i]

            pair(STEP * k, one)

        pair(STEP * k, force)

    for k in range(LAG):
        combine(k)
    reached = [0] * (ITERS + 1)
    for k in range(2):
        combine(k + LAG)
        gather(k)
        for n in range(1, ITERS + 1):
            goal = max(STEP * (k + 1) - (n - 1), 0)
            each(reached[n], goal, iterate(n))
            reached[n] = goal
    rim_g.wait_recv()

    def sweep(k, carry):
        @pl.when(k + LAG < count)
        def _():
            combine(k + LAG)

        gather(k)
        for n in range(1, ITERS + 1):
            pair(STEP * k - (n - 1), iterate(n))
        pass_on(k - 2).start()
        return carry

    lax.fori_loop(2, count, sweep, 0)
    rim_r.start()
    rim_r.wait_recv()
    each(planes, planes + HALO - 1, force)
    for n in range(1, ITERS + 1):
        each(planes - (n - 1), planes + ITERS - n, iterate(n))
    rim_s.start()
    pass_on(count - 2).start()
    pass_on(count - 1).start()

    @pl.when(odd == 1)
    def _():
        for m in range(relayed):
            detoured(m).wait_recv()
            forward(m).start()

    rim_s.wait_recv()

    def partial(k, carry):
        def one(i):
            res[i] = src[i] - diagonal[i] * (s2[i] - neighbours(s2, i))

        pair(STEP * k, one)
        return carry

    lax.fori_loop(0, count, partial, 0)

    def settle(m, carry):
        arrival(m).wait_recv()

        def one(i):
            res[i] = res[i] + p3[0, i]

        pair(STEP * m, one)
        return carry

    lax.fori_loop(0, count, settle, 0)

    def drain(k, carry):
        swap(k).wait_send()
        hand(k).wait_send()
        arrival(k).wait_send()
        return carry

    lax.fori_loop(0, count, drain, 0)

    @pl.when(odd == 1)
    def _():
        for m in range(relayed):
            forward(m).wait_send()

    for copy in rims + [rim_g, rim_r, rim_s]:
        copy.wait_send()


def finish(planes, s2, res, smoothed, residual, sem):
    copies = [
        pltpu.make_async_copy(s2.at[pl.ds(HALO, planes)], smoothed.at[0], sem.at[0]),
        pltpu.make_async_copy(res.at[pl.ds(HALO, planes)], residual.at[0], sem.at[1]),
    ]
    for copy in copies:
        copy.start()
    for copy in copies:
        copy.wait()


def body(steps, sides, initial, source, diffusion, advection):
    _, planes, rows, lanes = initial.shape
    assert sides == 2 and steps % 2 == 0 and planes % (2 * STEP) == 0
    count = planes // STEP
    relayed = 0
    shape = (planes + 2 * HALO, rows, lanes)
    wide = pltpu.VMEM(shape, jnp.float32)
    triple = pltpu.VMEM((3,) + shape, jnp.float32)
    double = pltpu.VMEM((2,) + shape, jnp.float32)
    dma = pltpu.SemaphoreType.DMA
    result = jax.ShapeDtypeStruct(initial.shape, jnp.float32)
    vmem = pl.BlockSpec(memory_space=pltpu.VMEM)
    hbm = pl.BlockSpec(memory_space=pltpu.HBM)
    grant = VMEM_BYTES - (2 * shape[0] + 4) * rows * lanes * 4
    held = pl.pallas_call(
        functools.partial(kernel, planes, steps, relayed),
        out_shape=(wide,) * 2,
        in_specs=[hbm] * 4,
        out_specs=(vmem,) * 2,
        scratch_shapes=[wide] * 3 + [triple] + [wide] * 23 + [double]
        + [dma((2, 4))] + [dma((count,))] * 5 + [dma((2, count)), dma((count,)), dma((7,)), dma((7,))],
        compiler_params=pltpu.CompilerParams(collective_id=0, has_side_effects=True, vmem_limit_bytes=grant),
        name="smooth",
    )(initial, source, diffusion, advection)
    return pl.pallas_call(
        functools.partial(finish, planes),
        out_shape=(result, result),
        in_specs=[vmem] * 2,
        out_specs=(hbm,) * 2,
        scratch_shapes=[dma((2,))],
        compiler_params=pltpu.CompilerParams(vmem_limit_bytes=8 << 20),
        name="finish",
    )(*held)


def solution(mesh):
    in_specs = (
        P("tm", "space", None, None),
        P("tm", "space", None, None),
        P("space", None, None),
        P(None, "space", None, None),
    )
    out_specs = (P("tm", "space", None, None), P("tm", "space", None, None))
    run = functools.partial(body, mesh.shape["tm"], mesh.shape["space"])
    return jax.shard_map(run, mesh=mesh, in_specs=in_specs, out_specs=out_specs, check_vma=False)
```

time: 44.6 us -> 40.6 us (0.910)
  the two profiles are of different devices: /device:TPU:0 before, /device:TPU:7 now
where the time goes in v1:
time: 40.6 us; the launch traced here: 40.5 us
  Pallas kernels  39.8 us (98%)
  between operations  0.64 us (2%)
    pallas_call x1, Pallas kernels, body(): pl.pallas_call(functools.partial(kernel, planes, steps, relayed), out_sha...  38.9 us
    pallas_call x1, Pallas kernels, body(): pl.pallas_call(functools.partial(finish, planes), out_shape=(result, resu...  0.99 us

profile of v1, /device:TPU:7, one launch (start us, length us, event | category | flops | bytes accessed | tf_op | source)
XLA Modules:
  0.0 40.5 jit_solution(15755306400907310280)
XLA Ops:
  0.6 38.9 %smooth.1 = (f32[24,64,128]{2,1,0:T(8,128)S(1)}, f32[24,64,128]{2,1,0:T(8,128)S(1)}) custom-call(f32[1,16,64,128]{3,2,1,0:T(8,128)} %initial.1, f32[1,16,64,128]{3,2,1,0:T(8,128)} %source.1, f32[16,64,128]{2,1,0:T(8,128)} %diffusion.1, f32[3,16,64,128]{3,2,1,0:T(8,128)} %advection.1), custom_call_target="tpu_custom_call" | custom-call | tf_op jit(solution)/shard_map/smooth/pallas_call | solution.py:350
  39.5 1.0 %finish.1 = (f32[1,16,64,128]{3,2,1,0:T(8,128)}, f32[1,16,64,128]{3,2,1,0:T(8,128)}) custom-call(f32[24,64,128]{2,1,0:T(8,128)S(1)} %get-tuple-element.4.s2, f32[24,64,128]{2,1,0:T(8,128)S(1)} %get-tuple-element.5.res), custom_call_target="tpu_custom_call" | custom-call | tf_op jit(solution)/shard_map/finish/pallas_call | solution.py:360

commit v2 on v1

--- a/solution.py
+++ b/solution.py
@@ -166,7 +166,7 @@
     def emit(k):
         swap(k).start()
 
-        @pl.when(odd == 1)
+        @pl.when(jnp.logical_and(odd == 1, k < relayed + 2))
         def _():
             hand(k).start()
 
@@ -265,6 +265,15 @@
         for n in range(1, ITERS + 1):
             pair(STEP * k - (n - 1), iterate(n))
         pass_on(k - 2).start()
+
+        @pl.when(jnp.logical_and(odd == 1, k == relayed + 1))
+        def _():
+            for m in range(relayed + 2, count):
+                hand(m).start()
+            for m in range(relayed):
+                detoured(m).wait_recv()
+                forward(m).start()
+
         return carry
 
     lax.fori_loop(2, count, sweep, 0)
@@ -277,12 +286,6 @@
     pass_on(count - 2).start()
     pass_on(count - 1).start()
 
-    @pl.when(odd == 1)
-    def _():
-        for m in range(relayed):
-            detoured(m).wait_recv()
-            forward(m).start()
-
     rim_s.wait_recv()
 
     def partial(k, carry):
@@ -337,7 +340,7 @@
     _, planes, rows, lanes = initial.shape
     assert sides == 2 and steps % 2 == 0 and planes % (2 * STEP) == 0
     count = planes // STEP
-    relayed = 0
+    relayed = 3
     shape = (planes + 2 * HALO, rows, lanes)
     wide = pltpu.VMEM(shape, jnp.float32)
     triple = pltpu.VMEM((3,) + shape, jnp.float32)

time: 40.6 us -> 35 us (0.86)
  the two profiles are of different devices: /device:TPU:7 before, /device:TPU:0 now
where the time goes in v2:
time: 35 us; the launch traced here: 34.8 us
  Pallas kernels  34.2 us (98%)
  between operations  0.64 us (2%)
    pallas_call x1, Pallas kernels, body(): pl.pallas_call(functools.partial(kernel, planes, steps, relayed), out_sha...  33.2 us
    pallas_call x1, Pallas kernels, body(): pl.pallas_call(functools.partial(finish, planes), out_shape=(result, resu...  0.99 us

profile of v2, /device:TPU:0, one launch (start us, length us, event | category | flops | bytes accessed | tf_op | source)
XLA Modules:
  0.0 34.8 jit_solution(3106332836935710710)
XLA Ops:
  0.6 33.2 %smooth.1 = (f32[24,64,128]{2,1,0:T(8,128)S(1)}, f32[24,64,128]{2,1,0:T(8,128)S(1)}) custom-call(f32[1,16,64,128]{3,2,1,0:T(8,128)} %initial.1, f32[1,16,64,128]{3,2,1,0:T(8,128)} %source.1, f32[16,64,128]{2,1,0:T(8,128)} %diffusion.1, f32[3,16,64,128]{3,2,1,0:T(8,128)} %advection.1), custom_call_target="tpu_custom_call" | custom-call | tf_op jit(solution)/shard_map/smooth/pallas_call | solution.py:353
  33.9 1.0 %finish.1 = (f32[1,16,64,128]{3,2,1,0:T(8,128)}, f32[1,16,64,128]{3,2,1,0:T(8,128)}) custom-call(f32[24,64,128]{2,1,0:T(8,128)S(1)} %get-tuple-element.4.s2, f32[24,64,128]{2,1,0:T(8,128)S(1)} %get-tuple-element.5.res), custom_call_target="tpu_custom_call" | custom-call | tf_op jit(solution)/shard_map/finish/pallas_call | solution.py:363

commit v3 on v2

--- a/solution.py
+++ b/solution.py
@@ -13,10 +13,14 @@
 LAG = 3
 VMEM_BYTES = 67043328
 MESH = pl.DeviceIdType.MESH
+EXTRA = 1
+REACH = [3, 3, 3, 3, 3]
+EARLY = [5, 8, 5, 5, 8, 0]
+ORDERS = [['', '', 'W5 W6 W7 F0 F1 F2', '', '', '', ''], ['', '', '', '', '', '', 'F1 F2'], ['', '', 'W5 W6 W7', '', 'F0', 'F1', 'F2'], ['', '', 'W5 W6 W7 F0 F1 F2', '', '', '', ''], ['', '', 'F0 F1 F2', '', '', '', ''], ['', '', '', '', '', 'G0', '']]
 
 
 def kernel(planes, steps, relayed, initial, source, diffusion, advection, s2, res,
-           u, src, spread, upwind, low_z, high_z, low_x, high_x, low_y, high_y, inverse, diagonal,
+           u, src, spread, upwind, low_z, low_x, low_y, even, inverse, diagonal,
            base, forced, y0, y1, y2, y3, v1, v2, v3, g, e, z, e_in, z_in, r, p3,
            load_sem, send_e, recv_e, send_z, recv_z, send_s, recv_s, send_f, hsend, hrecv):
     count = planes // STEP
@@ -41,9 +45,20 @@
     def part(k):
         return pl.ds(begin(STEP * k, STEP * k + STEP), STEP)
 
+    zone = odd - 1 + sum(
+        jnp.where(time == at, n, 0) for n, at in ((1, 1), (2, 3), (3, steps - 3), (4, steps - 1), (6, steps - 4)))
+    reach = sum(jnp.where(zone == n, REACH[n], 0) for n in range(len(REACH)))
+    lag = LAG + jnp.where(time == 0, LAG, 0)
+    early = sum(jnp.where(zone == n, EARLY[n], 0) for n in range(len(EARLY)))
+
     barrier = pltpu.get_barrier_semaphore()
     for peer in ((partner, side), (behind, side), (before, side), (time, other)):
         pl.semaphore_signal(barrier, inc=1, device_id=peer, device_id_type=MESH)
+    if EXTRA:
+        for here, there in ((0, steps - 4), (steps - 4, steps - 1)):
+            @pl.when(time == here)
+            def _():
+                pl.semaphore_signal(barrier, inc=1, device_id=(there, side), device_id_type=MESH)
 
     loads = []
     for n, (lo, hi) in enumerate(((0, half), (half, planes))):
@@ -91,21 +106,23 @@
             device_id=(beyond, side), device_id_type=MESH)
 
     def pass_on(m):
-        detour = odd * jnp.where(m < relayed, 1, 0)
-        return pltpu.make_async_remote_copy(
-            src_ref=s2.at[part(m)], dst_ref=p3.at[detour, part(m)], send_sem=send_s.at[m],
-            recv_sem=recv_s.at[detour, m],
-            device_id=(jnp.where(detour == 1, beyond, after), side), device_id_type=MESH)
-
-    def forward(m):
-        return pltpu.make_async_remote_copy(
-            src_ref=p3.at[1, part(m)], dst_ref=p3.at[0, part(m)], send_sem=send_f.at[m],
-            recv_sem=recv_s.at[0, m], device_id=(before, side), device_id_type=MESH)
-
-    def detoured(m):
-        return pltpu.make_async_remote_copy(
-            src_ref=s2.at[part(m)], dst_ref=p3.at[1, part(m)], send_sem=send_s.at[m],
-            recv_sem=recv_s.at[1, m], device_id=(beyond, side), device_id_type=MESH)
+        detour = odd * jnp.where(m < reach, 1, 0)
+        slot = detour * (1 + jnp.where(jnp.logical_and(zone == 4, m < EXTRA), 1, 0))
+        to = jnp.where(slot == 0, after, jnp.where(slot == 1, beyond, steps - 4))
+        return pltpu.make_async_remote_copy(
+            src_ref=s2.at[part(m)], dst_ref=p3.at[slot, part(m)], send_sem=send_s.at[m],
+            recv_sem=recv_s.at[slot, m], device_id=(to, side), device_id_type=MESH)
+
+    def forward(slot, m):
+        to = before if slot == 1 else 0
+        return pltpu.make_async_remote_copy(
+            src_ref=p3.at[slot, part(m)], dst_ref=p3.at[0, part(m)], send_sem=send_f.at[slot - 1, m],
+            recv_sem=recv_s.at[0, m], device_id=(to, side), device_id_type=MESH)
+
+    def detoured(slot, m):
+        return pltpu.make_async_remote_copy(
+            src_ref=s2.at[part(m)], dst_ref=p3.at[slot, part(m)], send_sem=send_s.at[m],
+            recv_sem=recv_s.at[slot, m], device_id=(beyond, side), device_id_type=MESH)
 
     def arrival(m):
         return pltpu.make_async_remote_copy(
@@ -124,18 +141,18 @@
 
     row = lax.broadcasted_iota(jnp.int32, (rows, lanes), 0)
     lane = lax.broadcasted_iota(jnp.int32, (rows, lanes), 1)
+    last_row = lax.broadcasted_iota(jnp.int32, (8, lanes), 0) == 7
+    last_lane = lane == lanes - 1
+    unit = 1 + jnp.minimum(time, 0)
 
     def coefficients(i):
         d = spread[i]
         ax, ay, az = upwind[0, i], upwind[1, i], upwind[2, i]
         main = 1.0 + 6.0 * d + (ax + ay + az)
         inv = 1.0 / main
-        even = d * inv
-        high_z[i] = even
+        even[i] = d * inv
         low_z[i] = (d + az) * inv
-        high_x[i] = jnp.where(row == rows - 1, 0.0, even)
         low_x[i] = jnp.where(row == 0, 0.0, (d + ax) * inv)
-        high_y[i] = jnp.where(lane == lanes - 1, 0.0, even)
         low_y[i] = jnp.where(lane == 0, 0.0, (d + ay) * inv)
         inverse[i] = inv
         diagonal[i] = main
@@ -143,10 +160,15 @@
         base[i] = src[i] * inv
 
     def neighbours(v, i):
+        flat = v.reshape(v.shape[0] * rows, lanes)
         here = v[i]
-        total = low_z[i] * v[i - 1] + high_z[i] * v[i + 1]
-        total += low_x[i] * pltpu.roll(here, 1, 0) + high_x[i] * pltpu.roll(here, rows - 1, 0)
-        return total + (low_y[i] * pltpu.roll(here, 1, 1) + high_y[i] * pltpu.roll(here, lanes - 1, 1))
+        below = flat[pl.ds(i * rows + unit, rows), :]
+        cut = rows - 8
+        below = jnp.concatenate([below[:cut], jnp.where(last_row, 0.0, below[cut:])], axis=0)
+        right = jnp.where(last_lane, 0.0, pltpu.roll(here, lanes - 1, 1))
+        total = even[i] * ((v[i + 1] + below) + right)
+        total += low_z[i] * v[i - 1] + low_x[i] * flat[pl.ds(i * rows - unit, rows), :]
+        return total + low_y[i] * pltpu.roll(here, 1, 1)
 
     powers, bases = [y0, y1, y2, y3], [u, v1, v2, v3]
 
@@ -166,7 +188,7 @@
     def emit(k):
         swap(k).start()
 
-        @pl.when(jnp.logical_and(odd == 1, k < relayed + 2))
+        @pl.when(jnp.logical_and(odd == 1, k < early))
         def _():
             hand(k).start()
 
@@ -175,7 +197,7 @@
     each(0, STEP + ITERS, coefficients)
     for n in range(1, ITERS + 1):
         each(0, STEP + ITERS - n, lift(n))
-    pl.semaphore_wait(barrier, 4)
+    pl.semaphore_wait(barrier, 4 + (jnp.where(zone >= 4, 1, 0) if EXTRA else 0))
     emit(0)
     for copy in rims:
         copy.start()
@@ -244,11 +266,25 @@
 
         pair(STEP * k, force)
 
+    def act(order):
+        for what in order.split():
+            n = int(what[1:])
+            if what[0] == "W":
+                hand(n).start()
+            else:
+                slot = 1 if what[0] == "F" else 2
+                detoured(slot, n).wait_recv()
+                forward(slot, n).start()
+
     for k in range(LAG):
         combine(k)
+    for k in range(LAG, 2 * LAG):
+        @pl.when(time == 0)
+        def _():
+            combine(k)
     reached = [0] * (ITERS + 1)
     for k in range(2):
-        combine(k + LAG)
+        combine(k + lag)
         gather(k)
         for n in range(1, ITERS + 1):
             goal = max(STEP * (k + 1) - (n - 1), 0)
@@ -257,22 +293,21 @@
     rim_g.wait_recv()
 
     def sweep(k, carry):
-        @pl.when(k + LAG < count)
-        def _():
-            combine(k + LAG)
+        @pl.when(k + lag < count)
+        def _():
+            combine(k + lag)
 
         gather(k)
         for n in range(1, ITERS + 1):
             pair(STEP * k - (n - 1), iterate(n))
         pass_on(k - 2).start()
 
-        @pl.when(jnp.logical_and(odd == 1, k == relayed + 1))
-        def _():
-            for m in range(relayed + 2, count):
-                hand(m).start()
-            for m in range(relayed):
-                detoured(m).wait_recv()
-                forward(m).start()
+        for where in range(len(ORDERS)):
+            for turn in range(2, count):
+                if ORDERS[where][turn - 2]:
+                    @pl.when(jnp.logical_and(zone == where, k == turn))
+                    def _():
+                        act(ORDERS[where][turn - 2])
 
         return carry
 
@@ -286,6 +321,12 @@
     pass_on(count - 2).start()
     pass_on(count - 1).start()
 
+    for where in range(len(ORDERS)):
+        if ORDERS[where][-1]:
+            @pl.when(zone == where)
+            def _():
+                act(ORDERS[where][-1])
+
     rim_s.wait_recv()
 
     def partial(k, carry):
@@ -316,10 +357,12 @@
 
     lax.fori_loop(0, count, drain, 0)
 
-    @pl.when(odd == 1)
-    def _():
-        for m in range(relayed):
-            forward(m).wait_send()
+    for where, order in enumerate(ORDERS):
+        @pl.when(zone == where)
+        def _():
+            for what in " ".join(order).split():
+                if what[0] != "W":
+                    forward(1 if what[0] == "F" else 2, int(what[1:])).wait_send()
 
     for copy in rims + [rim_g, rim_r, rim_s]:
         copy.wait_send()
@@ -344,7 +387,7 @@
     shape = (planes + 2 * HALO, rows, lanes)
     wide = pltpu.VMEM(shape, jnp.float32)
     triple = pltpu.VMEM((3,) + shape, jnp.float32)
-    double = pltpu.VMEM((2,) + shape, jnp.float32)
+    slots = pltpu.VMEM((3,) + shape, jnp.float32)
     dma = pltpu.SemaphoreType.DMA
     result = jax.ShapeDtypeStruct(initial.shape, jnp.float32)
     vmem = pl.BlockSpec(memory_space=pltpu.VMEM)
@@ -355,8 +398,8 @@
         out_shape=(wide,) * 2,
         in_specs=[hbm] * 4,
         out_specs=(vmem,) * 2,
-        scratch_shapes=[wide] * 3 + [triple] + [wide] * 23 + [double]
-        + [dma((2, 4))] + [dma((count,))] * 5 + [dma((2, count)), dma((count,)), dma((7,)), dma((7,))],
+        scratch_shapes=[wide] * 3 + [triple] + [wide] * 21 + [slots]
+        + [dma((2, 4))] + [dma((count,))] * 5 + [dma((3, count)), dma((2, count)), dma((7,)), dma((7,))],
         compiler_params=pltpu.CompilerParams(collective_id=0, has_side_effects=True, vmem_limit_bytes=grant),
         name="smooth",
     )(initial, source, diffusion, advection)

time: 35 us -> 34.2 us (0.977)
  Pallas kernels: 34.2 us -> 33.4 us
    pallas_call x1, Pallas kernels: 33.2 us -> 32.4 us  [body(): pl.pallas_call(functools.partial(kernel, planes, steps, relayed), out_sha...]
where the time goes in v3:
time: 34.2 us; the launch traced here: 34.1 us
  Pallas kernels  33.4 us (98%)
  between operations  0.64 us (2%)
    pallas_call x1, Pallas kernels, body(): pl.pallas_call(functools.partial(kernel, planes, steps, relayed), out_sha...  32.4 us
    pallas_call x1, Pallas kernels, body(): pl.pallas_call(functools.partial(finish, planes), out_shape=(result, resu...  0.99 us

profile of v3, /device:TPU:0, one launch (start us, length us, event | category | flops | bytes accessed | tf_op | source)
XLA Modules:
  0.0 34.1 jit_solution(14866083229497591069)
XLA Ops:
  0.6 32.4 %smooth.1 = (f32[24,64,128]{2,1,0:T(8,128)S(1)}, f32[24,64,128]{2,1,0:T(8,128)S(1)}) custom-call(f32[1,16,64,128]{3,2,1,0:T(8,128)} %initial.1, f32[1,16,64,128]{3,2,1,0:T(8,128)} %source.1, f32[16,64,128]{2,1,0:T(8,128)} %diffusion.1, f32[3,16,64,128]{3,2,1,0:T(8,128)} %advection.1), custom_call_target="tpu_custom_call" | custom-call | tf_op jit(solution)/shard_map/smooth/pallas_call | solution.py:396
  33.1 1.0 %finish.1 = (f32[1,16,64,128]{3,2,1,0:T(8,128)}, f32[1,16,64,128]{3,2,1,0:T(8,128)}) custom-call(f32[24,64,128]{2,1,0:T(8,128)S(1)} %get-tuple-element.4.s2, f32[24,64,128]{2,1,0:T(8,128)S(1)} %get-tuple-element.5.res), custom_call_target="tpu_custom_call" | custom-call | tf_op jit(solution)/shard_map/finish/pallas_call | solution.py:406

commit v4 on v3

--- a/solution.py
+++ b/solution.py
@@ -14,15 +14,22 @@
 VMEM_BYTES = 67043328
 MESH = pl.DeviceIdType.MESH
 EXTRA = 1
-REACH = [3, 3, 3, 3, 3]
+REACH = [3, 3, 3, 3, 4]
 EARLY = [5, 8, 5, 5, 8, 0]
-ORDERS = [['', '', 'W5 W6 W7 F0 F1 F2', '', '', '', ''], ['', '', '', '', '', '', 'F1 F2'], ['', '', 'W5 W6 W7', '', 'F0', 'F1', 'F2'], ['', '', 'W5 W6 W7 F0 F1 F2', '', '', '', ''], ['', '', 'F0 F1 F2', '', '', '', ''], ['', '', '', '', '', 'G0', '']]
-
-
-def kernel(planes, steps, relayed, initial, source, diffusion, advection, s2, res,
+ORDERS = [
+    [[], [], ["W5", "W6", "W7", "F0", "F1", "F2"], [], [], [], []],
+    [[], [], [], [], [], [], ["F1", "F2", "F3"]],
+    [[], [], ["W5", "W6", "W7"], [], ["F0"], ["F1"], ["F2"]],
+    [[], [], ["W5", "W6", "W7", "F0", "F1", "F2"], [], [], [], []],
+    [[], [], ["F0", "F1", "F2"], [], [], [], []],
+    [[], [], [], [], [], ["G0"], []],
+]
+
+
+def kernel(planes, steps, initial, source, diffusion, advection, s2, res,
            u, src, spread, upwind, low_z, low_x, low_y, even, inverse, diagonal,
            base, forced, y0, y1, y2, y3, v1, v2, v3, g, e, z, e_in, z_in, r, p3,
-           load_sem, send_e, recv_e, send_z, recv_z, send_s, recv_s, send_f, hsend, hrecv):
+           load_sem, sent, recv_e, recv_z, recv_s, hrecv):
     count = planes // STEP
     half = planes // 2
     time, side = lax.axis_index("tm"), lax.axis_index("space")
@@ -64,10 +71,10 @@
     for n, (lo, hi) in enumerate(((0, half), (half, planes))):
         here, there = span(lo, hi), grid_span(lo, hi)
         loads.append([
-            pltpu.make_async_copy(diffusion.at[there], spread.at[here], load_sem.at[n, 0]),
-            pltpu.make_async_copy(advection.at[:, there], upwind.at[:, here], load_sem.at[n, 1]),
-            pltpu.make_async_copy(initial.at[0, there], u.at[here], load_sem.at[n, 2]),
-            pltpu.make_async_copy(source.at[0, there], src.at[here], load_sem.at[n, 3]),
+            pltpu.make_async_copy(diffusion.at[there], spread.at[here], load_sem.at[n]),
+            pltpu.make_async_copy(advection.at[:, there], upwind.at[:, here], load_sem.at[n]),
+            pltpu.make_async_copy(initial.at[0, there], u.at[here], load_sem.at[n]),
+            pltpu.make_async_copy(source.at[0, there], src.at[here], load_sem.at[n]),
         ])
     for group in loads:
         for load in group:
@@ -79,7 +86,7 @@
 
     def across(source_ref, target_ref, n):
         return pltpu.make_async_remote_copy(
-            src_ref=source_ref, dst_ref=target_ref, send_sem=hsend.at[n], recv_sem=hrecv.at[n],
+            src_ref=source_ref, dst_ref=target_ref, send_sem=sent.at[1], recv_sem=hrecv.at[n],
             device_id=(time, other), device_id_type=MESH)
 
     def rim(field, width, n):
@@ -89,45 +96,56 @@
     mine, theirs = grid_span(planes - HALO, planes), span(planes, planes + HALO, other)
     rims = [
         across(diffusion.at[mine], spread.at[theirs], 0),
-        across(advection.at[:, mine], upwind.at[:, theirs], 1),
-        across(initial.at[0, mine], u.at[theirs], 2),
-        across(source.at[0, mine], src.at[theirs], 3),
+        across(advection.at[:, mine], upwind.at[:, theirs], 0),
+        across(initial.at[0, mine], u.at[theirs], 0),
+        across(source.at[0, mine], src.at[theirs], 0),
     ]
-    rim_g, rim_r, rim_s = rim(g, HALO, 4), rim(r, HALO - 1, 5), rim(s2, 1, 6)
+    rim_g, rim_r, rim_s = rim(g, HALO, 1), rim(r, HALO - 1, 2), rim(s2, 1, 3)
 
     def swap(k):
         return pltpu.make_async_remote_copy(
-            src_ref=e.at[part(k)], dst_ref=e_in.at[part(k)], send_sem=send_e.at[k], recv_sem=recv_e.at[k],
+            src_ref=e.at[part(k)], dst_ref=e_in.at[part(k)], send_sem=sent.at[0], recv_sem=recv_e.at[k],
             device_id=(partner, side), device_id_type=MESH)
 
     def hand(k):
         return pltpu.make_async_remote_copy(
-            src_ref=z.at[part(k)], dst_ref=z_in.at[part(k)], send_sem=send_z.at[k], recv_sem=recv_z.at[k],
+            src_ref=z.at[part(k)], dst_ref=z_in.at[part(k)], send_sem=sent.at[0], recv_sem=recv_z.at[k],
             device_id=(beyond, side), device_id_type=MESH)
+
+    depth = planes + 2 * HALO
+
+    def place(slot, m):
+        return p3.at[pl.ds(slot * depth + begin(STEP * m, STEP * m + STEP), STEP)]
+
+    def landed(slot, m):
+        return recv_s.at[slot * count - jnp.where(slot == 2, count - max(REACH), 0) + m]
 
     def pass_on(m):
         detour = odd * jnp.where(m < reach, 1, 0)
         slot = detour * (1 + jnp.where(jnp.logical_and(zone == 4, m < EXTRA), 1, 0))
         to = jnp.where(slot == 0, after, jnp.where(slot == 1, beyond, steps - 4))
         return pltpu.make_async_remote_copy(
-            src_ref=s2.at[part(m)], dst_ref=p3.at[slot, part(m)], send_sem=send_s.at[m],
-            recv_sem=recv_s.at[slot, m], device_id=(to, side), device_id_type=MESH)
+            src_ref=s2.at[part(m)], dst_ref=place(slot, m), send_sem=sent.at[0],
+            recv_sem=landed(slot, m), device_id=(to, side), device_id_type=MESH)
 
     def forward(slot, m):
         to = before if slot == 1 else 0
         return pltpu.make_async_remote_copy(
-            src_ref=p3.at[slot, part(m)], dst_ref=p3.at[0, part(m)], send_sem=send_f.at[slot - 1, m],
-            recv_sem=recv_s.at[0, m], device_id=(to, side), device_id_type=MESH)
-
-    def detoured(slot, m):
-        return pltpu.make_async_remote_copy(
-            src_ref=s2.at[part(m)], dst_ref=p3.at[slot, part(m)], send_sem=send_s.at[m],
-            recv_sem=recv_s.at[slot, m], device_id=(beyond, side), device_id_type=MESH)
-
-    def arrival(m):
-        return pltpu.make_async_remote_copy(
-            src_ref=s2.at[part(m)], dst_ref=p3.at[0, part(m)], send_sem=send_s.at[m],
-            recv_sem=recv_s.at[0, m], device_id=(after, side), device_id_type=MESH)
+            src_ref=place(slot, m), dst_ref=place(0, m), send_sem=sent.at[2],
+            recv_sem=landed(0, m), device_id=(to, side), device_id_type=MESH)
+
+    def arrival(slot, m):
+        return pltpu.make_async_remote_copy(
+            src_ref=s2.at[part(m)], dst_ref=place(slot, m), send_sem=sent.at[0],
+            recv_sem=landed(slot, m), device_id=(after, side), device_id_type=MESH)
+
+    def loaded(n, amount):
+        return pltpu.make_async_copy(p3.at[pl.ds(0, amount)], p3.at[pl.ds(0, amount)], load_sem.at[n])
+
+    def total(n, amount):
+        return pltpu.make_async_remote_copy(
+            src_ref=p3.at[pl.ds(0, amount)], dst_ref=p3.at[pl.ds(0, amount)], send_sem=sent.at[n],
+            recv_sem=hrecv.at[0], device_id=(time, other), device_id_type=MESH)
 
     def each(lo, hi, body):
         start = begin(lo, hi)
@@ -172,7 +190,7 @@
 
     powers, bases = [y0, y1, y2, y3], [u, v1, v2, v3]
 
-    def lift(n):
+    def lift(n, whole=True):
         def one(i):
             y = neighbours(powers[n - 1], i)
             b = base[i] + neighbours(bases[n - 1], i)
@@ -182,8 +200,22 @@
             else:
                 g[i] = b
                 e[i] = b + diagonal[i] * y
-                z[i] = (y0[i] + y1[i]) + (y2[i] + y3[i])
+                if whole:
+                    spread_sum(i)
         return one
+
+    def raise_power(n):
+        def one(i):
+            powers[n][i] = neighbours(powers[n - 1], i)
+        return one
+
+    def raise_base(n):
+        def one(i):
+            bases[n][i] = base[i] + neighbours(bases[n - 1], i)
+        return one
+
+    def spread_sum(i):
+        z[i] = (y0[i] + y1[i]) + (y2[i] + y3[i])
 
     def emit(k):
         swap(k).start()
@@ -192,13 +224,21 @@
         def _():
             hand(k).start()
 
-    for load in loads[0]:
-        load.wait()
+    loaded(0, 6 * half).wait()
     each(0, STEP + ITERS, coefficients)
-    for n in range(1, ITERS + 1):
-        each(0, STEP + ITERS - n, lift(n))
+    for n in range(1, ITERS):
+        each(0, STEP + ITERS - n, raise_power(n))
+    each(0, STEP, spread_sum)
     pl.semaphore_wait(barrier, 4 + (jnp.where(zone >= 4, 1, 0) if EXTRA else 0))
-    emit(0)
+
+    @pl.when(odd == 1)
+    def _():
+        hand(0).start()
+
+    for n in range(1, ITERS):
+        each(0, STEP + ITERS - n, raise_base(n))
+    each(0, STEP, lift(ITERS, False))
+    swap(0).start()
     for copy in rims:
         copy.start()
 
@@ -207,13 +247,11 @@
 
         @pl.when(lo + ITERS == half)
         def _():
-            for load in loads[1]:
-                load.wait()
+            loaded(1, 6 * (planes - half)).wait()
 
         @pl.when(lo + ITERS == planes)
         def _():
-            for copy in rims:
-                copy.wait_recv()
+            total(1, 6 * HALO).wait_recv()
 
         pair(lo + ITERS, coefficients)
         for n in range(1, ITERS + 1):
@@ -267,13 +305,13 @@
         pair(STEP * k, force)
 
     def act(order):
-        for what in order.split():
+        for what in order:
             n = int(what[1:])
             if what[0] == "W":
                 hand(n).start()
             else:
                 slot = 1 if what[0] == "F" else 2
-                detoured(slot, n).wait_recv()
+                arrival(slot, n).wait_recv()
                 forward(slot, n).start()
 
     for k in range(LAG):
@@ -318,8 +356,14 @@
     for n in range(1, ITERS + 1):
         each(planes - (n - 1), planes + ITERS - n, iterate(n))
     rim_s.start()
-    pass_on(count - 2).start()
-    pass_on(count - 1).start()
+
+    def close():
+        pass_on(count - 2).start()
+        pass_on(count - 1).start()
+
+    @pl.when(zone != 1)
+    def _():
+        close()
 
     for where in range(len(ORDERS)):
         if ORDERS[where][-1]:
@@ -327,6 +371,10 @@
             def _():
                 act(ORDERS[where][-1])
 
+    @pl.when(zone == 1)
+    def _():
+        close()
+
     rim_s.wait_recv()
 
     def partial(k, carry):
@@ -339,33 +387,24 @@
     lax.fori_loop(0, count, partial, 0)
 
     def settle(m, carry):
-        arrival(m).wait_recv()
-
-        def one(i):
-            res[i] = res[i] + p3[0, i]
+        arrival(0, m).wait_recv()
+
+        def one(i):
+            res[i] = res[i] + p3[i]
 
         pair(STEP * m, one)
         return carry
 
     lax.fori_loop(0, count, settle, 0)
 
-    def drain(k, carry):
-        swap(k).wait_send()
-        hand(k).wait_send()
-        arrival(k).wait_send()
-        return carry
-
-    lax.fori_loop(0, count, drain, 0)
-
+    total(0, 3 * planes).wait_send()
+    total(1, 8 * HALO).wait_send()
     for where, order in enumerate(ORDERS):
-        @pl.when(zone == where)
-        def _():
-            for what in " ".join(order).split():
-                if what[0] != "W":
-                    forward(1 if what[0] == "F" else 2, int(what[1:])).wait_send()
-
-    for copy in rims + [rim_g, rim_r, rim_s]:
-        copy.wait_send()
+        passed = sum(what[0] != "W" for what in sum(order, []))
+        if passed:
+            @pl.when(zone == where)
+            def _():
+                total(2, STEP * passed).wait_send()
 
 
 def finish(planes, s2, res, smoothed, residual, sem):
@@ -383,23 +422,23 @@
     _, planes, rows, lanes = initial.shape
     assert sides == 2 and steps % 2 == 0 and planes % (2 * STEP) == 0
     count = planes // STEP
-    relayed = 3
     shape = (planes + 2 * HALO, rows, lanes)
     wide = pltpu.VMEM(shape, jnp.float32)
     triple = pltpu.VMEM((3,) + shape, jnp.float32)
-    slots = pltpu.VMEM((3,) + shape, jnp.float32)
+    slots = pltpu.VMEM((3 * shape[0],) + shape[1:], jnp.float32)
     dma = pltpu.SemaphoreType.DMA
     result = jax.ShapeDtypeStruct(initial.shape, jnp.float32)
     vmem = pl.BlockSpec(memory_space=pltpu.VMEM)
     hbm = pl.BlockSpec(memory_space=pltpu.HBM)
     grant = VMEM_BYTES - (2 * shape[0] + 4) * rows * lanes * 4
     held = pl.pallas_call(
-        functools.partial(kernel, planes, steps, relayed),
+        functools.partial(kernel, planes, steps),
         out_shape=(wide,) * 2,
         in_specs=[hbm] * 4,
         out_specs=(vmem,) * 2,
         scratch_shapes=[wide] * 3 + [triple] + [wide] * 21 + [slots]
-        + [dma((2, 4))] + [dma((count,))] * 5 + [dma((3, count)), dma((2, count)), dma((7,)), dma((7,))],
+        + [dma((2,)), dma((3,))] + [dma((count,))] * 2
+        + [dma((count + max(REACH) + EXTRA,)), dma((4,))],
         compiler_params=pltpu.CompilerParams(collective_id=0, has_side_effects=True, vmem_limit_bytes=grant),
         name="smooth",
     )(initial, source, diffusion, advection)

time: 34.2 us -> 33.3 us (0.974)
  Pallas kernels: 33.4 us -> 32.5 us
    pallas_call x1, Pallas kernels: 32.4 us -> 31.5 us  [body(): pl.pallas_call(functools.partial(kernel, planes, steps), out_shape=(wide,...]
where the time goes in v4:
time: 33.3 us; the launch traced here: 33.1 us
  Pallas kernels  32.5 us (98%)
  between operations  0.64 us (2%)
    pallas_call x1, Pallas kernels, body(): pl.pallas_call(functools.partial(kernel, planes, steps), out_shape=(wide,...  31.5 us
    pallas_call x1, Pallas kernels, body(): pl.pallas_call(functools.partial(finish, planes), out_shape=(result, resu...  0.99 us

profile of v4, /device:TPU:0, one launch (start us, length us, event | category | flops | bytes accessed | tf_op | source)
XLA Modules:
  0.0 33.1 jit_solution(16651632369853996175)
XLA Ops:
  0.6 31.5 %smooth.1 = (f32[24,64,128]{2,1,0:T(8,128)S(1)}, f32[24,64,128]{2,1,0:T(8,128)S(1)}) custom-call(f32[1,16,64,128]{3,2,1,0:T(8,128)} %initial.1, f32[1,16,64,128]{3,2,1,0:T(8,128)} %source.1, f32[16,64,128]{2,1,0:T(8,128)} %diffusion.1, f32[3,16,64,128]{3,2,1,0:T(8,128)} %advection.1), custom_call_target="tpu_custom_call" | custom-call | tf_op jit(solution)/shard_map/smooth/pallas_call | solution.py:434
  32.1 1.0 %finish.1 = (f32[1,16,64,128]{3,2,1,0:T(8,128)}, f32[1,16,64,128]{3,2,1,0:T(8,128)}) custom-call(f32[24,64,128]{2,1,0:T(8,128)S(1)} %get-tuple-element.4.s2, f32[24,64,128]{2,1,0:T(8,128)S(1)} %get-tuple-element.5.res), custom_call_target="tpu_custom_call" | custom-call | tf_op jit(solution)/shard_map/finish/pallas_call | solution.py:445

commit v5 on v4

--- a/solution.py
+++ b/solution.py
@@ -13,16 +13,18 @@
 LAG = 3
 VMEM_BYTES = 67043328
 MESH = pl.DeviceIdType.MESH
-EXTRA = 1
-REACH = [3, 3, 3, 3, 4]
-EARLY = [5, 8, 5, 5, 8, 0]
+REACH = [3, 3, 3, 2, 0]
+ROUND = ((2, 0), (2, 1), (1, 0), (1, 0), (1, 0), (0, 0), (0, 0), (0, 0))
+EARLY = [5, 8, 5, 5, 8]
 ORDERS = [
     [[], [], ["W5", "W6", "W7", "F0", "F1", "F2"], [], [], [], []],
-    [[], [], [], [], [], [], ["F1", "F2", "F3"]],
+    [[], [], [], [], [], [], ["F2", "F3", "F4"]],
     [[], [], ["W5", "W6", "W7"], [], ["F0"], ["F1"], ["F2"]],
     [[], [], ["W5", "W6", "W7", "F0", "F1", "F2"], [], [], [], []],
-    [[], [], ["F0", "F1", "F2"], [], [], [], []],
-    [[], [], [], [], [], ["G0"], []],
+    [[], [], ["F0", "F1"], [], [], [], []],
+    [[], [], [], ["G0"], [], [], []],
+    [[], [], [], ["G1"], [], [], []],
+    [[], [], [], [], [], [], []],
 ]
 
 
@@ -53,7 +55,7 @@
         return pl.ds(begin(STEP * k, STEP * k + STEP), STEP)
 
     zone = odd - 1 + sum(
-        jnp.where(time == at, n, 0) for n, at in ((1, 1), (2, 3), (3, steps - 3), (4, steps - 1), (6, steps - 4)))
+        jnp.where(time == at, n, 0) for n, at in ((1, 1), (2, 3), (3, steps - 3), (4, steps - 1), (6, steps - 4), (7, steps - 2)))
     reach = sum(jnp.where(zone == n, REACH[n], 0) for n in range(len(REACH)))
     lag = LAG + jnp.where(time == 0, LAG, 0)
     early = sum(jnp.where(zone == n, EARLY[n], 0) for n in range(len(EARLY)))
@@ -61,11 +63,14 @@
     barrier = pltpu.get_barrier_semaphore()
     for peer in ((partner, side), (behind, side), (before, side), (time, other)):
         pl.semaphore_signal(barrier, inc=1, device_id=peer, device_id_type=MESH)
-    if EXTRA:
-        for here, there in ((0, steps - 4), (steps - 4, steps - 1)):
+    guests = (steps - 4,)
+    for guest in guests:
+        for here, there in ((0, guest), (guest, steps - 1)):
             @pl.when(time == here)
             def _():
                 pl.semaphore_signal(barrier, inc=1, device_id=(there, side), device_id_type=MESH)
+
+    greeted = 4 + sum(jnp.where(zone == n, extra, 0) for n, extra in ((4, 1), (5, 1)))
 
     loads = []
     for n, (lo, hi) in enumerate(((0, half), (half, planes))):
@@ -118,12 +123,14 @@
         return p3.at[pl.ds(slot * depth + begin(STEP * m, STEP * m + STEP), STEP)]
 
     def landed(slot, m):
-        return recv_s.at[slot * count - jnp.where(slot == 2, count - max(REACH), 0) + m]
+        return recv_s.at[jnp.where(slot == 0, m, count + jnp.where(slot == 1, m % 4, 4 + m % 2))]
 
     def pass_on(m):
-        detour = odd * jnp.where(m < reach, 1, 0)
-        slot = detour * (1 + jnp.where(jnp.logical_and(zone == 4, m < EXTRA), 1, 0))
-        to = jnp.where(slot == 0, after, jnp.where(slot == 1, beyond, steps - 4))
+        near = jnp.where(m < reach, 1, 0)
+        far = sum(jnp.where(m == n, slot, 0) for n, (slot, _) in enumerate(ROUND))
+        slot = odd * jnp.where(zone == 4, far, near)
+        host = sum(jnp.where(m == n, (steps - 4, steps - 2)[at], 0) for n, (slot_, at) in enumerate(ROUND) if slot_ == 2)
+        to = jnp.where(slot == 0, after, jnp.where(slot == 1, beyond, host))
         return pltpu.make_async_remote_copy(
             src_ref=s2.at[part(m)], dst_ref=place(slot, m), send_sem=sent.at[0],
             recv_sem=landed(slot, m), device_id=(to, side), device_id_type=MESH)
@@ -229,7 +236,7 @@
     for n in range(1, ITERS):
         each(0, STEP + ITERS - n, raise_power(n))
     each(0, STEP, spread_sum)
-    pl.semaphore_wait(barrier, 4 + (jnp.where(zone >= 4, 1, 0) if EXTRA else 0))
+    pl.semaphore_wait(barrier, greeted)
 
     @pl.when(odd == 1)
     def _():
@@ -408,14 +415,15 @@
 
 
 def finish(planes, s2, res, smoothed, residual, sem):
-    copies = [
-        pltpu.make_async_copy(s2.at[pl.ds(HALO, planes)], smoothed.at[0], sem.at[0]),
-        pltpu.make_async_copy(res.at[pl.ds(HALO, planes)], residual.at[0], sem.at[1]),
-    ]
+    size = planes // 2
+    copies = []
+    for lo in range(0, planes, size):
+        copies.append(pltpu.make_async_copy(s2.at[pl.ds(HALO + lo, size)], smoothed.at[0, pl.ds(lo, size)], sem.at[0]))
+        copies.append(pltpu.make_async_copy(res.at[pl.ds(HALO + lo, size)], residual.at[0, pl.ds(lo, size)], sem.at[1]))
     for copy in copies:
         copy.start()
-    for copy in copies:
-        copy.wait()
+    pltpu.make_async_copy(s2.at[pl.ds(HALO, planes)], smoothed.at[0], sem.at[0]).wait()
+    pltpu.make_async_copy(res.at[pl.ds(HALO, planes)], residual.at[0], sem.at[1]).wait()
 
 
 def body(steps, sides, initial, source, diffusion, advection):
@@ -438,7 +446,7 @@
         out_specs=(vmem,) * 2,
         scratch_shapes=[wide] * 3 + [triple] + [wide] * 21 + [slots]
         + [dma((2,)), dma((3,))] + [dma((count,))] * 2
-        + [dma((count + max(REACH) + EXTRA,)), dma((4,))],
+        + [dma((count + 6,)), dma((4,))],
         compiler_params=pltpu.CompilerParams(collective_id=0, has_side_effects=True, vmem_limit_bytes=grant),
         name="smooth",
     )(initial, source, diffusion, advection)

time: 33.3 us -> 32.5 us (0.976)
  Pallas kernels: 32.5 us -> 31.7 us
    pallas_call x1, Pallas kernels: 31.5 us -> 30.8 us  [body(): pl.pallas_call(functools.partial(kernel, planes, steps), out_shape=(wide,...]
where the time goes in v5:
time: 32.5 us; the launch traced here: 32.4 us
  Pallas kernels  31.7 us (98%)
  between operations  0.64 us (2%)
    pallas_call x1, Pallas kernels, body(): pl.pallas_call(functools.partial(kernel, planes, steps), out_shape=(wide,...  30.8 us
    pallas_call x1, Pallas kernels, body(): pl.pallas_call(functools.partial(finish, planes), out_shape=(result, resu...  0.98 us

profile of v5, /device:TPU:0, one launch (start us, length us, event | category | flops | bytes accessed | tf_op | source)
XLA Modules:
  0.0 32.4 jit_solution(10060516816672008566)
XLA Ops:
  0.6 30.8 %smooth.1 = (f32[24,64,128]{2,1,0:T(8,128)S(1)}, f32[24,64,128]{2,1,0:T(8,128)S(1)}) custom-call(f32[1,16,64,128]{3,2,1,0:T(8,128)} %initial.1, f32[1,16,64,128]{3,2,1,0:T(8,128)} %source.1, f32[16,64,128]{2,1,0:T(8,128)} %diffusion.1, f32[3,16,64,128]{3,2,1,0:T(8,128)} %advection.1), custom_call_target="tpu_custom_call" | custom-call | tf_op jit(solution)/shard_map/smooth/pallas_call | solution.py:442
  31.4 1.0 %finish.1 = (f32[1,16,64,128]{3,2,1,0:T(8,128)}, f32[1,16,64,128]{3,2,1,0:T(8,128)}) custom-call(f32[24,64,128]{2,1,0:T(8,128)S(1)} %get-tuple-element.4.s2, f32[24,64,128]{2,1,0:T(8,128)S(1)} %get-tuple-element.5.res), custom_call_target="tpu_custom_call" | custom-call | tf_op jit(solution)/shard_map/finish/pallas_call | solution.py:453

commit v6 on v5

--- a/solution.py
+++ b/solution.py
@@ -23,8 +23,7 @@
     [[], [], ["W5", "W6", "W7", "F0", "F1", "F2"], [], [], [], []],
     [[], [], ["F0", "F1"], [], [], [], []],
     [[], [], [], ["G0"], [], [], []],
-    [[], [], [], ["G1"], [], [], []],
-    [[], [], [], [], [], [], []],
+    [[], [], ["G1"], [], [], [], []],
 ]
 
 
@@ -33,7 +32,7 @@
            base, forced, y0, y1, y2, y3, v1, v2, v3, g, e, z, e_in, z_in, r, p3,
            load_sem, sent, recv_e, recv_z, recv_s, hrecv):
     count = planes // STEP
-    half = planes // 2
+    half = STEP + ITERS
     time, side = lax.axis_index("tm"), lax.axis_index("space")
     odd = lax.rem(time, 2)
     partner = time + 1 - 2 * odd
@@ -428,7 +427,7 @@
 
 def body(steps, sides, initial, source, diffusion, advection):
     _, planes, rows, lanes = initial.shape
-    assert sides == 2 and steps % 2 == 0 and planes % (2 * STEP) == 0
+    assert sides == 2 and steps % 2 == 0 and steps >= 8 and planes % (2 * STEP) == 0
     count = planes // STEP
     shape = (planes + 2 * HALO, rows, lanes)
     wide = pltpu.VMEM(shape, jnp.float32)

time: 32.5 us -> 32.5 us (level)
  no operation moved by 1% of the time
where the time goes in v6:
time: 32.5 us; the launch traced here: 32.3 us
  Pallas kernels  31.7 us (98%)
  between operations  0.64 us (2%)
    pallas_call x1, Pallas kernels, body(): pl.pallas_call(functools.partial(kernel, planes, steps), out_shape=(wide,...  30.7 us
    pallas_call x1, Pallas kernels, body(): pl.pallas_call(functools.partial(finish, planes), out_shape=(result, resu...  0.98 us

profile of v6, /device:TPU:0, one launch (start us, length us, event | category | flops | bytes accessed | tf_op | source)
XLA Modules:
  0.0 32.3 jit_solution(16888536323968648185)
XLA Ops:
  0.6 30.7 %smooth.1 = (f32[24,64,128]{2,1,0:T(8,128)S(1)}, f32[24,64,128]{2,1,0:T(8,128)S(1)}) custom-call(f32[1,16,64,128]{3,2,1,0:T(8,128)} %initial.1, f32[1,16,64,128]{3,2,1,0:T(8,128)} %source.1, f32[16,64,128]{2,1,0:T(8,128)} %diffusion.1, f32[3,16,64,128]{3,2,1,0:T(8,128)} %advection.1), custom_call_target="tpu_custom_call" | custom-call | tf_op jit(solution)/shard_map/smooth/pallas_call | solution.py:441
  31.3 1.0 %finish.1 = (f32[1,16,64,128]{3,2,1,0:T(8,128)}, f32[1,16,64,128]{3,2,1,0:T(8,128)}) custom-call(f32[24,64,128]{2,1,0:T(8,128)S(1)} %get-tuple-element.4.s2, f32[24,64,128]{2,1,0:T(8,128)S(1)} %get-tuple-element.5.res), custom_call_target="tpu_custom_call" | custom-call | tf_op jit(solution)/shard_map/finish/pallas_call | solution.py:452

commit v7 on v6

--- a/solution.py
+++ b/solution.py
@@ -122,7 +122,7 @@
         return p3.at[pl.ds(slot * depth + begin(STEP * m, STEP * m + STEP), STEP)]
 
     def landed(slot, m):
-        return recv_s.at[jnp.where(slot == 0, m, count + jnp.where(slot == 1, m % 4, 4 + m % 2))]
+        return recv_s.at[jnp.where(slot == 0, jnp.maximum(m - (count - 3), 0), 3 + jnp.where(slot == 1, m % 4, 4 + m % 2))]
 
     def pass_on(m):
         near = jnp.where(m < reach, 1, 0)
@@ -392,8 +392,15 @@
 
     lax.fori_loop(0, count, partial, 0)
 
+    bulk = STEP * (count - 2)
+    pltpu.make_async_remote_copy(
+        src_ref=p3.at[pl.ds(0, bulk)], dst_ref=p3.at[pl.ds(0, bulk)], send_sem=sent.at[0],
+        recv_sem=recv_s.at[0], device_id=(after, side), device_id_type=MESH).wait_recv()
+
     def settle(m, carry):
-        arrival(0, m).wait_recv()
+        @pl.when(m >= count - 2)
+        def _():
+            arrival(0, m).wait_recv()
 
         def one(i):
             res[i] = res[i] + p3[i]
@@ -445,7 +452,7 @@
         out_specs=(vmem,) * 2,
         scratch_shapes=[wide] * 3 + [triple] + [wide] * 21 + [slots]
         + [dma((2,)), dma((3,))] + [dma((count,))] * 2
-        + [dma((count + 6,)), dma((4,))],
+        + [dma((9,)), dma((4,))],
         compiler_params=pltpu.CompilerParams(collective_id=0, has_side_effects=True, vmem_limit_bytes=grant),
         name="smooth",
     )(initial, source, diffusion, advection)

time: 32.5 us -> 32.4 us (level)
  no operation moved by 1% of the time
where the time goes in v7:
time: 32.4 us; the launch traced here: 32.3 us
  Pallas kernels  31.6 us (98%)
  between operations  0.64 us (2%)
    pallas_call x1, Pallas kernels, body(): pl.pallas_call(functools.partial(kernel, planes, steps), out_shape=(wide,...  30.6 us
    pallas_call x1, Pallas kernels, body(): pl.pallas_call(functools.partial(finish, planes), out_shape=(result, resu...  0.98 us

profile of v7, /device:TPU:0, one launch (start us, length us, event | category | flops | bytes accessed | tf_op | source)
XLA Modules:
  0.0 32.3 jit_solution(323341821704804501)
XLA Ops:
  0.6 30.6 %smooth.1 = (f32[24,64,128]{2,1,0:T(8,128)S(1)}, f32[24,64,128]{2,1,0:T(8,128)S(1)}) custom-call(f32[1,16,64,128]{3,2,1,0:T(8,128)} %initial.1, f32[1,16,64,128]{3,2,1,0:T(8,128)} %source.1, f32[16,64,128]{2,1,0:T(8,128)} %diffusion.1, f32[3,16,64,128]{3,2,1,0:T(8,128)} %advection.1), custom_call_target="tpu_custom_call" | custom-call | tf_op jit(solution)/shard_map/smooth/pallas_call | solution.py:448
  31.3 1.0 %finish.1 = (f32[1,16,64,128]{3,2,1,0:T(8,128)}, f32[1,16,64,128]{3,2,1,0:T(8,128)}) custom-call(f32[24,64,128]{2,1,0:T(8,128)S(1)} %get-tuple-element.4.s2, f32[24,64,128]{2,1,0:T(8,128)S(1)} %get-tuple-element.5.res), custom_call_target="tpu_custom_call" | custom-call | tf_op jit(solution)/shard_map/finish/pallas_call | solution.py:459
